TPU v7x, 32 devices: a whole 2x2x4 slice. The times are simulated.
32 devices in a mesh: group: 2 (over x), tp: 4 (over z), dp: 4 (over y, core).
Axes of the slice: x: 2, y: 2, z: 4, core: 2. Of those that a mesh axis runs over, the one named last changes fastest.
Arguments:
- image_slots: bfloat16 [128, 8192], P(('group', 'tp'), 'dp'), may hold values from -6 to 6
- image_cot: bfloat16 [128, 8192], P(('group', 'tp'), 'dp'), may hold values from -6 to 6
- text_rows: bfloat16 [64, 8192], P(('group', 'tp'), 'dp'), may hold values from -6 to 6
- text_cot: bfloat16 [64, 8192], P(('group', 'tp'), 'dp'), may hold values from -6 to 6
- destination: int32 [64, 1], P(('group', 'tp')), may hold values from 0 to 1; in each aligned block of 8 rows (0 to 7, 8 to 15, ...) at most 8 rows name the same one
- text_count: int32 [8], P(('group', 'tp')), may hold values from 1 to 8, 48 in all
- w_gate: bfloat16 [8192, 14336], P('dp', 'tp'), may hold values from -0.0625 to 0.0625
- w_up: bfloat16 [8192, 14336], P('dp', 'tp'), may hold values from -0.0625 to 0.0625
- w_down: bfloat16 [14336, 8192], P('tp', 'dp'), may hold values from -0.046875 to 0.046875
Outputs:
- image_grad: bfloat16 [64, 8192], P(('group', 'tp'), 'dp')
- text_grad: bfloat16 [64, 8192], P(('group', 'tp'), 'dp')
Inputs may be any that keep to these rules, and one draw needn't show every extreme that they name: In the rows of one block of 8 rows no group is named more than 8 times, and some block names one group exactly 8 times; destination[i] decides which slot of image_slots and image_cot holds row i. Each block of 8 text rows has text_count live rows first; some block is full.
All inputs are finite; a program needn't handle non-finite values.
Results may differ from a plain program's by a relative error of at most 0.025.
Values may be sent and summed in bfloat16 or wider, within the bound.
No kernel may reach another device: no remote copies, remote signals or barrier semaphores. Data moves between devices by JAX's collectives and lax.ppermute only.
A program may use at most 128 MiB of HBM per device.

v0:
```python
import jax
import jax.numpy as jnp
from jax import lax
from jax.sharding import PartitionSpec as P


def language_grads(combined, w_gate, w_up, w_down):
    feat_dev = w_gate.shape[0]
    hidden_dev = w_gate.shape[1]
    piece = lax.all_gather(combined, "tp", axis=0, tiled=True)
    inputs_part = piece[:, :feat_dev]
    cot_part = piece[:, feat_dev:]
    gate = jnp.dot(inputs_part, w_gate, preferred_element_type=jnp.float32)
    up = jnp.dot(inputs_part, w_up, preferred_element_type=jnp.float32)
    back = lax.dot_general(
        cot_part, w_down, (((1,), (1,)), ((), ())), preferred_element_type=jnp.float32
    )
    partial_value = jnp.concatenate([gate, up, back], axis=1)
    sums = lax.psum_scatter(
        partial_value.astype(jnp.bfloat16), "dp", scatter_dimension=0, tiled=True
    ).astype(jnp.float32)
    gate = sums[:, :hidden_dev]
    up = sums[:, hidden_dev : 2 * hidden_dev]
    back = sums[:, 2 * hidden_dev :]
    sigmoid_gate = jax.nn.sigmoid(gate)
    dgate = (back * up * sigmoid_gate * (1.0 + gate * (1.0 - sigmoid_gate))).astype(jnp.bfloat16)
    dup = (back * gate * sigmoid_gate).astype(jnp.bfloat16)
    stacked = jnp.concatenate([dgate, dup], axis=1)
    piece = lax.all_gather(stacked, "dp", axis=0, tiled=True)
    total = lax.dot_general(
        piece[:, :hidden_dev], w_gate, (((1,), (1,)), ((), ())), preferred_element_type=jnp.float32
    )
    terms = total + lax.dot_general(
        piece[:, hidden_dev:], w_up, (((1,), (1,)), ((), ())), preferred_element_type=jnp.float32
    )
    return lax.psum_scatter(terms.astype(jnp.bfloat16), "tp", scatter_dimension=0, tiled=True)


def per_device(
    image_slots, image_cot, text_rows, text_cot, destination, text_count, w_gate, w_up, w_down
):
    groups = lax.axis_size("group")
    slot_dev = image_slots.shape[0]
    capacity = slot_dev // groups
    image_dev = destination.shape[0]
    text_dev = text_rows.shape[0]
    target = destination[:, 0]
    position = lax.broadcasted_iota(jnp.int32, (image_dev, image_dev), 0)
    other = lax.broadcasted_iota(jnp.int32, (image_dev, image_dev), 1)
    same = (target[:, None] == target[None, :]) & (other < position)
    rank = jnp.sum(same.astype(jnp.int32), axis=1)
    column = target * capacity + rank
    slot_index = lax.broadcasted_iota(jnp.int32, (image_dev, slot_dev), 1)
    select = (column[:, None] == slot_index).astype(jnp.bfloat16)
    text_both = jnp.concatenate([text_rows, text_cot], axis=1)
    both = jnp.concatenate([image_slots, image_cot], axis=1)
    arrived = lax.all_to_all(both, "group", split_axis=0, concat_axis=0, tiled=True)
    picked = jnp.dot(select, arrived, preferred_element_type=jnp.float32).astype(jnp.bfloat16)
    combined = jnp.concatenate([picked, text_both], axis=0)
    grads = language_grads(combined, w_gate, w_up, w_down)
    image_grad = grads[:image_dev]
    text_part = grads[image_dev:]
    live = lax.broadcasted_iota(jnp.int32, (text_dev, 1), 0) < text_count[0]
    text_grad = jnp.where(live, text_part, jnp.zeros_like(text_part))
    return (image_grad, text_grad)


def solution(mesh):
    placed = (
        P(("group", "tp"), "dp"),
        P(("group", "tp"), "dp"),
        P(("group", "tp"), "dp"),
        P(("group", "tp"), "dp"),
        P(("group", "tp"), None),
        P(("group", "tp")),
        P("dp", "tp"),
        P("dp", "tp"),
        P("tp", "dp"),
    )
    return jax.shard_map(
        per_device,
        mesh=mesh,
        in_specs=placed,
        out_specs=(P(("group", "tp"), "dp"), P(("group", "tp"), "dp")),
        check_vma=False,
    )
```

profile of v0, /device:TPU:0, one launch (start us, length us, event | category | flops | bytes accessed | tf_op | source)
XLA Modules:
  0.0 142.4 jit_solution(585150537257338750)
XLA Ops:
  7.2 1.5 %maximum_bitcast_fusion = bf16[2,8,4096]{2,1,0:T(8,128)(2,1)} fusion(bf16[16,2048]{1,0:T(8,128)(2,1)} %param.10, bf16[16,2048]{1,0:T(8,128)(2,1)} %param.9), kind=kLoop, calls=%fused_computation.20 | loop fusion | flops 262144 | bytes 262144 | tf_op jit(solution)/shard_map/all_to_all | solution.py:57
  8.7 4.2 %all-to-all-start = ((bf16[2,8,4096]{2,1,0:T(8,128)(2,1)}), bf16[2,8,4096]{2,1,0:T(8,128)(2,1)S(1)}, u32[]{:S(2)}, u32[]{:S(2)}) async-start(bf16[2,8,4096]{2,1,0:T(8,128)(2,1)} %maximum_bitcast_fusion), calls=%async_computation | async-start | bytes 262144 | tf_op jit(solution)/shard_map/all_to_all | solution.py:57
  12.9 0.0 reduce-scatter.3.cloned.1.call-start
  12.9 0.9 convert_reduce_fusion
  13.8 0.7 fusion.13
  14.5 3.0 %all-to-all-done = bf16[2,8,4096]{2,1,0:T(8,128)(2,1)S(1)} async-done(((bf16[2,8,4096]{2,1,0:T(8,128)(2,1)}), bf16[2,8,4096]{2,1,0:T(8,128)(2,1)S(1)}, u32[]{:S(2)}, u32[]{:S(2)}) %all-to-all-start) | async-done | bytes 131104 | tf_op jit(solution)/shard_map/all_to_all | solution.py:57
  17.5 0.2 convolution_convert_fusion.3
  17.7 0.8 maximum_maximum_fusion
  18.5 15.6 %all_gather.6 = bf16[64,4096]{1,0:T(8,128)(2,1)S(1)} all-gather(bf16[16,4096]{1,0:T(8,128)(2,1)S(1)} %maximum_maximum_fusion), channel_id=1, replica_groups=mesh['group'=2,'tp'=4,'dp'=4] {'tp'}, dimensions={0}, use_global_device_ids=true | all-gather | bytes 655360 | tf_op jit(solution)/shard_map/all_gather | solution.py:10
  34.1 0.0 slice-start
  34.1 0.0 slice-start.1
  34.1 9.9 %convolution_convert_fusion = bf16[64,3584]{1,0:T(8,128)(2,1)S(1)} fusion(bf16[3584,2048]{1,0:T(8,128)(2,1)} %param.17, bf16[64,4096]{1,0:T(8,128)(2,1)S(1)} %all_gather.6), kind=kOutput, calls=%fused_computation | convolution fusion | flops 939753472 | bytes 15400960 | tf_op jit(solution)/shard_map/dot_general | solution.py:15
  43.9 0.0 slice-start.2
  43.9 0.0 slice-start.3
  44.0 8.0 %convolution_convert_fusion.1 = bf16[64,3584]{1,0:T(8,128)(2,1)S(1)} fusion(bf16[2048,3584]{1,0:T(8,128)(2,1)} %param.16, bf16[64,4096]{1,0:T(8,128)(2,1)S(1)} %all_gather.6), kind=kOutput, calls=%fused_computation.1 | convolution fusion | flops 939753472 | bytes 15400960 | tf_op jit(solution)/shard_map/dot_general | solution.py:14
  51.9 0.0 slice-done
  51.9 0.0 slice-done.1
  51.9 0.0 slice-done.2
  51.9 0.0 slice-done.3
  52.0 2.6 %convolution_convert_fusion.2 = bf16[64,3584]{1,0:T(8,128)(2,1)S(1)} fusion(bf16[2048,3584]{1,0:T(8,128)(2,1)S(1)} %bitcast.20, bf16[64,4096]{1,0:T(8,128)(2,1)S(1)} %all_gather.6), kind=kOutput, calls=%fused_computation.2 | convolution fusion | flops 939753472 | bytes 15400960 | tf_op jit(solution)/shard_map/dot_general | solution.py:13
  54.6 1.2 pad_maximum_fusion
  55.8 0.0 reduce-scatter.3.cloned.1.call-update
  55.8 0.0 reduce-scatter.5.cloned.1.call-start
  55.9 27.5 %reduce-scatter.3.cloned.1.call-done = bf16[16,10752]{1,0:T(8,128)(2,1)} async-done(((bf16[64,10752]{1,0:T(8,128)(2,1)}), bf16[16,10752]{1,0:T(8,128)(2,1)}) %reduce-scatter.3.cloned.1.call-update) | async-done | bytes 344080 | tf_op jit(solution)/shard_map/reduce_scatter | solution.py:19
  83.4 1.0 convert_element_type.22
  84.4 0.1 fusion.9
  84.6 8.7 %all_gather.7 = bf16[64,7168]{1,0:T(8,128)(2,1)S(1)} all-gather(bf16[16,7168]{1,0:T(8,128)(2,1)S(1)} %pad_maximum_fusion.1), channel_id=1, replica_groups=mesh['group'=2,'tp'=4,'dp'=4] {'dp'}, dimensions={0}, use_global_device_ids=true | all-gather | bytes 1146880 | tf_op jit(solution)/shard_map/all_gather | solution.py:29
  93.3 9.7 %fusion.2 = f32[64,2048]{1,0:T(8,128)S(1)} fusion(bf16[2048,3584]{1,0:T(8,128)(2,1)} %param.15, bf16[64,7168]{1,0:T(8,128)(2,1)S(1)} %all_gather.7), kind=kOutput, calls=%fused_computation.8 | convolution fusion | flops 939524096 | bytes 15663104 | tf_op jit(solution)/shard_map/dot_general | solution.py:30
  102.9 10.4 %fusion = bf16[64,2048]{1,0:T(8,128)(2,1)} fusion(f32[64,2048]{1,0:T(8,128)S(1)} %fusion.2, bf16[2048,3584]{1,0:T(8,128)(2,1)} %param.16, bf16[64,7168]{1,0:T(8,128)(2,1)S(1)} %all_gather.7), kind=kOutput, calls=%fused_computation.5 | convolution fusion | flops 939786240 | bytes 15925248 | tf_op jit(solution)/shard_map/dot_general | solution.py:33
  113.3 0.0 reduce-scatter.5.cloned.1.call-update
  114.0 20.1 %reduce-scatter.5.cloned.1.call-done = bf16[16,2048]{1,0:T(8,128)(2,1)} async-done(((bf16[64,2048]{1,0:T(8,128)(2,1)}), bf16[16,2048]{1,0:T(8,128)(2,1)}) %reduce-scatter.5.cloned.1.call-update) | async-done | bytes 65552 | tf_op jit(solution)/shard_map/reduce_scatter | solution.py:36
  134.1 1.5 %slice_select_fusion = (bf16[8,2048]{1,0:T(8,128)(2,1)}, bf16[8,2048]{1,0:T(8,128)(2,1)}) fusion(bf16[16,2048]{1,0:T(8,128)(2,1)} %reduce-scatter.5.cloned.1.call-done, pred[8]{0:T(512)(128)(4,1)S(1)} %iota_compare_fusion.3), kind=kLoop, calls=%fused_computation.23 | loop fusion | flops 16384 | bytes 131080 | tf_op jit(solution)/shard_map/jit(_where)/select_n | solution.py:64
  (3 shorter events, 0.0 us)
Async XLA Ops:
  8.7 8.8 %all-to-all-start = ((bf16[2,8,4096]{2,1,0:T(8,128)(2,1)}), bf16[2,8,4096]{2,1,0:T(8,128)(2,1)S(1)}, u32[]{:S(2)}, u32[]{:S(2)}) async-start(bf16[2,8,4096]{2,1,0:T(8,128)(2,1)} %maximum_bitcast_fusion), calls=%async_computation | async-start | bytes 262144 | tf_op jit(solution)/shard_map/all_to_all | solution.py:57
  12.9 70.5 %reduce-scatter.3.cloned.1.call-start = ((), (), s32[]{:S(2)}) async-start(), calls=%async_computation.3 | async-start | bytes 1720320 | tf_op jit(solution)/shard_map/reduce_scatter | solution.py:19
  34.1 17.8 %slice-start = ((s8[14680064]{0:T(1024)(128)(4,1)}), s8[4194304]{0:T(1024)(128)(4,1)S(1)}, s32[]{:S(2)}) async-start(s8[14680064]{0:T(1024)(128)(4,1)} %bitcast.19), calls=%async_computation.5 | async-start | bytes 8388608
  34.1 17.9 %slice-start.1 = ((s8[14680064]{0:T(1024)(128)(4,1)}), s8[2097152]{0:T(1024)(128)(4,1)S(1)}, s32[]{:S(2)}) async-start(s8[14680064]{0:T(1024)(128)(4,1)} %bitcast.19), calls=%async_computation.6 | async-start | bytes 4194304
  43.9 8.0 %slice-start.2 = ((s8[14680064]{0:T(1024)(128)(4,1)}), s8[4194304]{0:T(1024)(128)(4,1)S(1)}, s32[]{:S(2)}) async-start(s8[14680064]{0:T(1024)(128)(4,1)} %bitcast.19), calls=%async_computation.7 | async-start | bytes 8388608
  43.9 8.0 %slice-start.3 = ((s8[14680064]{0:T(1024)(128)(4,1)}), s8[4194304]{0:T(1024)(128)(4,1)S(1)}, s32[]{:S(2)}) async-start(s8[14680064]{0:T(1024)(128)(4,1)} %bitcast.19), calls=%async_computation.8 | async-start | bytes 8388608
  55.8 78.3 %reduce-scatter.5.cloned.1.call-start = ((), (), s32[]{:S(2)}) async-start(), calls=%async_computation.4 | async-start | bytes 327680 | tf_op jit(solution)/shard_map/reduce_scatter | solution.py:36
Sparse Core Ops, SparseCore 0:
  55.9 27.4 reduce-scatter.2
  113.5 20.5 reduce-scatter.4
where the time goes:
time: 143 us; the launch traced here: 142 us
  waiting for transfers between devices  50.6 us (35%)
  matrix products  40.7 us (28%)
  blocking collectives  24.3 us (17%)
  between operations  14.8 us (10%)
  other arithmetic  7.71 us (5%)
  starting transfers between devices  4.28 us (3%)
    reduce_scatter x1, waiting for transfers between devices, language_grads(): lax.psum_scatter(partial_value.astype(jnp.bfloat16), 'dp', scatter_dimens...  27.5 us
    reduce_scatter x1, waiting for transfers between devices, language_grads(): lax.psum_scatter(terms.astype(jnp.bfloat16), 'tp', scatter_dimension=0, t...  20.1 us
    all_gather x1, blocking collectives, language_grads(): piece = lax.all_gather(combined, 'tp', axis=0, tiled=True)  15.6 us
    dot_general x1, matrix products, language_grads(): lax.dot_general(piece[:, hidden_dev:], w_up, (((1,), (1,)), ((), ())), pr...  10.4 us
    dot_general x1, matrix products, language_grads(): lax.dot_general(cot_part, w_down, (((1,), (1,)), ((), ())), preferred_ele...  9.86 us
    dot_general x1, matrix products, language_grads(): lax.dot_general(piece[:, :hidden_dev], w_gate, (((1,), (1,)), ((), ())),...  9.67 us
    all_gather x1, blocking collectives, language_grads(): piece = lax.all_gather(stacked, 'dp', axis=0, tiled=True)  8.72 us
    dot_general x1, matrix products, language_grads(): up = jnp.dot(inputs_part, w_up, preferred_element_type=jnp.float32)  7.95 us
  transfers between devices with their start and end apart: 3, of which 3 were waited for; matrix products, arithmetic and copies ran while one was open for 1% of the time, Pallas kernels for 0%

commit v1 on v0

--- a/solution.py
+++ b/solution.py
@@ -2,6 +2,16 @@
 import jax.numpy as jnp
 from jax import lax
 from jax.sharding import PartitionSpec as P
+
+
+def gather_by_hops(array, axis, dim):
+    n_dev = lax.axis_size(axis)
+    held, pieces = (array, [array])
+    for _ in range(n_dev - 1):
+        held = lax.ppermute(held, axis, [(i, (i + 1) % n_dev) for i in range(n_dev)])
+        pieces.insert(0, held)
+    row_of_blocks = jnp.concatenate(pieces, axis=dim)
+    return jnp.roll(row_of_blocks, (lax.axis_index(axis) + 1) * array.shape[dim], axis=dim)
 
 
 def language_grads(combined, w_gate, w_up, w_down):
@@ -26,7 +36,7 @@
     dgate = (back * up * sigmoid_gate * (1.0 + gate * (1.0 - sigmoid_gate))).astype(jnp.bfloat16)
     dup = (back * gate * sigmoid_gate).astype(jnp.bfloat16)
     stacked = jnp.concatenate([dgate, dup], axis=1)
-    piece = lax.all_gather(stacked, "dp", axis=0, tiled=True)
+    piece = gather_by_hops(stacked, "dp", 0)
     total = lax.dot_general(
         piece[:, :hidden_dev], w_gate, (((1,), (1,)), ((), ())), preferred_element_type=jnp.float32
     )

time: 143 us -> 150 us (1.049)
  waiting for transfers between devices: 50.6 us -> 66.4 us
  blocking collectives: 24.3 us -> 15.6 us
    ppermute x0 -> x3, waiting for transfers between devices: none -> 16.3 us  [gather_by_hops(): lax.ppermute(held, axis, [(i, (i + 1) % n_dev) for i in range(n_dev)])]
    all_gather x1 -> x0, blocking collectives: 8.72 us -> none  [language_grads(): piece = lax.all_gather(stacked, 'dp', axis=0, tiled=True)]
  transfers between devices with their start and end apart: 3 -> 6, of which waited for: 3 -> 6; matrix products, arithmetic and copies ran while one was open for 1% -> 1% of each run, Pallas kernels for 0% -> 0%
where the time goes in v1:
time: 150 us
  waiting for transfers between devices  66.4 us (44%)
  matrix products  40.7 us (27%)
  blocking collectives  15.6 us (10%)
  between operations  14.8 us (10%)
  other arithmetic  7.75 us (5%)
  starting transfers between devices  4.34 us (3%)
    reduce_scatter x1, waiting for transfers between devices, language_grads(): lax.psum_scatter(partial_value.astype(jnp.bfloat16), 'dp', scatter_dimens...  27.5 us
    reduce_scatter x1, waiting for transfers between devices, language_grads(): lax.psum_scatter(terms.astype(jnp.bfloat16), 'tp', scatter_dimension=0, t...  19.5 us
    ppermute x3, waiting for transfers between devices, gather_by_hops(): lax.ppermute(held, axis, [(i, (i + 1) % n_dev) for i in range(n_dev)])  16.3 us
    all_gather x1, blocking collectives, language_grads(): piece = lax.all_gather(combined, 'tp', axis=0, tiled=True)  15.6 us
    dot_general x1, matrix products, language_grads(): lax.dot_general(piece[:, :hidden_dev], w_gate, (((1,), (1,)), ((), ())),...  10.4 us
    dot_general x1, matrix products, language_grads(): lax.dot_general(cot_part, w_down, (((1,), (1,)), ((), ())), preferred_ele...  9.86 us
    dot_general x1, matrix products, language_grads(): lax.dot_general(piece[:, hidden_dev:], w_up, (((1,), (1,)), ((), ())), pr...  9.67 us
    dot_general x1, matrix products, language_grads(): up = jnp.dot(inputs_part, w_up, preferred_element_type=jnp.float32)  7.96 us
  transfers between devices with their start and end apart: 6, of which 6 were waited for; matrix products, arithmetic and copies ran while one was open for 1% of the time, Pallas kernels for 0%

profile of v1, /device:TPU:0, one launch (start us, length us, event | category | flops | bytes accessed | tf_op | source)
XLA Modules:
  0.0 149.7 jit_solution(3277791591593666196)
XLA Ops:
  7.2 1.5 %maximum_bitcast_fusion = bf16[2,8,4096]{2,1,0:T(8,128)(2,1)} fusion(bf16[16,2048]{1,0:T(8,128)(2,1)} %param.10, bf16[16,2048]{1,0:T(8,128)(2,1)} %param.9), kind=kLoop, calls=%fused_computation.20 | loop fusion | flops 262144 | bytes 262144 | tf_op jit(solution)/shard_map/all_to_all | solution.py:67
  8.7 4.2 %all-to-all-start = ((bf16[2,8,4096]{2,1,0:T(8,128)(2,1)}), bf16[2,8,4096]{2,1,0:T(8,128)(2,1)S(1)}, u32[]{:S(2)}, u32[]{:S(2)}) async-start(bf16[2,8,4096]{2,1,0:T(8,128)(2,1)} %maximum_bitcast_fusion), calls=%async_computation | async-start | bytes 262144 | tf_op jit(solution)/shard_map/all_to_all | solution.py:67
  12.9 0.0 reduce-scatter.3.cloned.1.call-start
  12.9 0.9 convert_reduce_fusion
  13.8 0.7 fusion.13
  14.5 3.0 %all-to-all-done = bf16[2,8,4096]{2,1,0:T(8,128)(2,1)S(1)} async-done(((bf16[2,8,4096]{2,1,0:T(8,128)(2,1)}), bf16[2,8,4096]{2,1,0:T(8,128)(2,1)S(1)}, u32[]{:S(2)}, u32[]{:S(2)}) %all-to-all-start) | async-done | bytes 131104 | tf_op jit(solution)/shard_map/all_to_all | solution.py:67
  17.5 0.2 convolution_convert_fusion.3
  17.7 0.8 maximum_maximum_fusion
  18.5 15.6 %all_gather.3 = bf16[64,4096]{1,0:T(8,128)(2,1)S(1)} all-gather(bf16[16,4096]{1,0:T(8,128)(2,1)S(1)} %maximum_maximum_fusion), channel_id=1, replica_groups=mesh['group'=2,'tp'=4,'dp'=4] {'tp'}, dimensions={0}, use_global_device_ids=true | all-gather | bytes 655360 | tf_op jit(solution)/shard_map/all_gather | solution.py:20
  34.1 0.0 slice-start
  34.1 0.0 slice-start.1
  34.1 9.9 %convolution_convert_fusion = bf16[64,3584]{1,0:T(8,128)(2,1)S(1)} fusion(bf16[3584,2048]{1,0:T(8,128)(2,1)} %param.17, bf16[64,4096]{1,0:T(8,128)(2,1)S(1)} %all_gather.3), kind=kOutput, calls=%fused_computation | convolution fusion | flops 939753472 | bytes 15400960 | tf_op jit(solution)/shard_map/dot_general | solution.py:25
  43.9 0.0 slice-start.2
  44.0 0.0 slice-start.3
  44.0 8.0 %convolution_convert_fusion.1 = bf16[64,3584]{1,0:T(8,128)(2,1)S(1)} fusion(bf16[2048,3584]{1,0:T(8,128)(2,1)} %param.16, bf16[64,4096]{1,0:T(8,128)(2,1)S(1)} %all_gather.3), kind=kOutput, calls=%fused_computation.1 | convolution fusion | flops 939753472 | bytes 15400960 | tf_op jit(solution)/shard_map/dot_general | solution.py:24
  51.9 0.0 slice-done
  51.9 0.0 slice-done.1
  51.9 0.0 slice-done.2
  51.9 0.0 slice-done.3
  52.0 2.6 %convolution_convert_fusion.2 = bf16[64,3584]{1,0:T(8,128)(2,1)S(1)} fusion(bf16[2048,3584]{1,0:T(8,128)(2,1)S(1)} %bitcast.20, bf16[64,4096]{1,0:T(8,128)(2,1)S(1)} %all_gather.3), kind=kOutput, calls=%fused_computation.2 | convolution fusion | flops 939753472 | bytes 15400960 | tf_op jit(solution)/shard_map/dot_general | solution.py:23
  54.6 1.2 pad_maximum_fusion
  55.8 0.0 reduce-scatter.3.cloned.1.call-update
  55.8 0.0 reduce-scatter.5.cloned.1.call-start
  55.9 27.5 %reduce-scatter.3.cloned.1.call-done = bf16[16,10752]{1,0:T(8,128)(2,1)} async-done(((bf16[64,10752]{1,0:T(8,128)(2,1)}), bf16[16,10752]{1,0:T(8,128)(2,1)}) %reduce-scatter.3.cloned.1.call-update) | async-done | bytes 344080 | tf_op jit(solution)/shard_map/reduce_scatter | solution.py:29
  83.4 1.0 convert_element_type.22
  84.4 0.1 fusion.9
  84.6 0.1 collective-permute-start
  84.6 5.4 %collective-permute-done = bf16[16,7168]{1,0:T(8,128)(2,1)S(1)} collective-permute-done((bf16[16,7168]{1,0:T(8,128)(2,1)S(1)}, bf16[16,7168]{1,0:T(8,128)(2,1)S(1)}, u32[]{:S(2)}, u32[]{:S(2)}) %collective-permute-start) | collective-permute-done | bytes 229408 | tf_op jit(solution)/shard_map/ppermute | solution.py:11
  90.1 0.0 collective-permute-start.1
  90.1 5.4 %collective-permute-done.1 = bf16[16,7168]{1,0:T(8,128)(2,1)S(1)} collective-permute-done((bf16[16,7168]{1,0:T(8,128)(2,1)S(1)}, bf16[16,7168]{1,0:T(8,128)(2,1)S(1)}, u32[]{:S(2)}, u32[]{:S(2)}) %collective-permute-start.1) | collective-permute-done | bytes 229408 | tf_op jit(solution)/shard_map/ppermute | solution.py:11
  95.5 0.0 collective-permute-start.2
  95.5 5.4 %collective-permute-done.2 = bf16[16,7168]{1,0:T(8,128)(2,1)S(1)} collective-permute-done((bf16[16,7168]{1,0:T(8,128)(2,1)S(1)}, bf16[16,7168]{1,0:T(8,128)(2,1)S(1)}, u32[]{:S(2)}, u32[]{:S(2)}) %collective-permute-start.2) | collective-permute-done | bytes 229408 | tf_op jit(solution)/shard_map/ppermute | solution.py:11
  101.2 9.7 %fusion.1 = f32[64,2048]{1,0:T(8,128)S(1)} fusion(bf16[2048,3584]{1,0:T(8,128)(2,1)} %param.16, bf16[128,7168]{1,0:T(8,128)(2,1)S(1)} %constant_dynamic-update-slice_fusion, s32[]{:T(128)S(6)} %select_n.18, s32[]{:T(128)S(6)} %add.37), kind=kOutput, calls=%fused_computation.7 | convolution fusion | flops 939524096 | bytes 15663112 | tf_op jit(solution)/shard_map/dot_general | solution.py:43
  110.8 10.4 %fusion = bf16[64,2048]{1,0:T(8,128)(2,1)} fusion(f32[64,2048]{1,0:T(8,128)S(1)} %fusion.1, bf16[2048,3584]{1,0:T(8,128)(2,1)} %param.15, bf16[128,7168]{1,0:T(8,128)(2,1)S(1)} %constant_dynamic-update-slice_fusion, s32[]{:T(128)S(6)} %select_n.18), kind=kOutput, calls=%fused_computation.5 | convolution fusion | flops 939786240 | bytes 15925252 | tf_op jit(solution)/shard_map/dot_general | solution.py:40
  121.2 0.0 reduce-scatter.5.cloned.1.call-update
  121.9 19.5 %reduce-scatter.5.cloned.1.call-done = bf16[16,2048]{1,0:T(8,128)(2,1)} async-done(((bf16[64,2048]{1,0:T(8,128)(2,1)}), bf16[16,2048]{1,0:T(8,128)(2,1)}) %reduce-scatter.5.cloned.1.call-update) | async-done | bytes 65552 | tf_op jit(solution)/shard_map/reduce_scatter | solution.py:46
  141.4 1.5 slice_select_fusion
  (11 shorter events, 0.2 us)
Async XLA Ops:
  8.7 8.8 %all-to-all-start = ((bf16[2,8,4096]{2,1,0:T(8,128)(2,1)}), bf16[2,8,4096]{2,1,0:T(8,128)(2,1)S(1)}, u32[]{:S(2)}, u32[]{:S(2)}) async-start(bf16[2,8,4096]{2,1,0:T(8,128)(2,1)} %maximum_bitcast_fusion), calls=%async_computation | async-start | bytes 262144 | tf_op jit(solution)/shard_map/all_to_all | solution.py:67
  12.9 70.5 %reduce-scatter.3.cloned.1.call-start = ((), (), s32[]{:S(2)}) async-start(), calls=%async_computation.3 | async-start | bytes 1720320 | tf_op jit(solution)/shard_map/reduce_scatter | solution.py:29
  34.1 17.8 %slice-start = ((s8[14680064]{0:T(1024)(128)(4,1)}), s8[4194304]{0:T(1024)(128)(4,1)S(1)}, s32[]{:S(2)}) async-start(s8[14680064]{0:T(1024)(128)(4,1)} %bitcast.19), calls=%async_computation.5 | async-start | bytes 8388608
  34.1 17.9 %slice-start.1 = ((s8[14680064]{0:T(1024)(128)(4,1)}), s8[2097152]{0:T(1024)(128)(4,1)S(1)}, s32[]{:S(2)}) async-start(s8[14680064]{0:T(1024)(128)(4,1)} %bitcast.19), calls=%async_computation.6 | async-start | bytes 4194304
  43.9 8.0 %slice-start.2 = ((s8[14680064]{0:T(1024)(128)(4,1)}), s8[4194304]{0:T(1024)(128)(4,1)S(1)}, s32[]{:S(2)}) async-start(s8[14680064]{0:T(1024)(128)(4,1)} %bitcast.19), calls=%async_computation.7 | async-start | bytes 8388608
  44.0 8.0 %slice-start.3 = ((s8[14680064]{0:T(1024)(128)(4,1)}), s8[4194304]{0:T(1024)(128)(4,1)S(1)}, s32[]{:S(2)}) async-start(s8[14680064]{0:T(1024)(128)(4,1)} %bitcast.19), calls=%async_computation.8 | async-start | bytes 8388608
  55.8 85.6 %reduce-scatter.5.cloned.1.call-start = ((), (), s32[]{:S(2)}) async-start(), calls=%async_computation.4 | async-start | bytes 327680 | tf_op jit(solution)/shard_map/reduce_scatter | solution.py:46
  84.6 5.5 %collective-permute-start = (bf16[16,7168]{1,0:T(8,128)(2,1)S(1)}, bf16[16,7168]{1,0:T(8,128)(2,1)S(1)}, u32[]{:S(2)}, u32[]{:S(2)}) collective-permute-start(bf16[16,7168]{1,0:T(8,128)(2,1)S(1)} %pad_maximum_fusion.1), channel_id=1, source_target_pairs={{0,1},{1,2},{2,3},{3,0},{4,5},{5,6},{6,7},{7,4},{8,9},{9,10},{10,1... | collective-permute-start | bytes 688136 | tf_op jit(solution)/shard_map/ppermute | solution.py:11
  90.1 5.4 %collective-permute-start.1 = (bf16[16,7168]{1,0:T(8,128)(2,1)S(1)}, bf16[16,7168]{1,0:T(8,128)(2,1)S(1)}, u32[]{:S(2)}, u32[]{:S(2)}) collective-permute-start(bf16[16,7168]{1,0:T(8,128)(2,1)S(1)} %collective-permute-done), channel_id=1, source_target_pairs={{0,1},{1,2},{2,3},{3,0},{4,5},{5,6},{6,7},{7,4},{8,9},{9,10},{10,1... | collective-permute-start | bytes 688136 | tf_op jit(solution)/shard_map/ppermute | solution.py:11
  95.5 5.4 %collective-permute-start.2 = (bf16[16,7168]{1,0:T(8,128)(2,1)S(1)}, bf16[16,7168]{1,0:T(8,128)(2,1)S(1)}, u32[]{:S(2)}, u32[]{:S(2)}) collective-permute-start(bf16[16,7168]{1,0:T(8,128)(2,1)S(1)} %collective-permute-done.1), channel_id=1, source_target_pairs={{0,1},{1,2},{2,3},{3,0},{4,5},{5,6},{6,7},{7,4},{8,9},{9,10},{10,1... | collective-permute-start | bytes 688136 | tf_op jit(solution)/shard_map/ppermute | solution.py:11
Sparse Core Ops, SparseCore 0:
  55.9 27.4 reduce-scatter.2
  121.4 19.9 reduce-scatter.4
